TPU v7x, 32 devices: a whole 2x2x4 slice. The times are simulated.
32 devices in a mesh: region: 2 (over y), member: 8 (over z, core), space: 2 (over x).
Axes of the slice: x: 2, y: 2, z: 4, core: 2. Of those that a mesh axis runs over, the one named last changes fastest.
Arguments:
- prior_trials: bfloat16 [80, 1536, 256], P('member', ('region', 'space')), parts along dimension 1, may hold values from -6 to 6
- prior_at_sensors: bfloat16 [80, 1536], P('member', ('region', 'space')), parts along dimension 1, may hold values from -6 to 6
- sensor_readings: bfloat16 [1536], P(('region', 'space')), parts along dimension 0, may hold values from -8 to 8
- sensor_noise_spread: bfloat16 [1536], P(('region', 'space')), parts along dimension 0, may hold values from 1 to 10
- nearby_readings: int32 [1536, 128], P(('region', 'space')), parts along dimension 0, may hold values from 0 to 1023, as said below
- subarea_cutoff_level: int32 [1536], P(('region', 'space')), parts along dimension 0, may hold values from 0 to 3
Outputs:
- analysis: bfloat16 [80, 1536, 256], P('member', ('region', 'space')), parts along dimension 1
There are 2 independent parts, one for each index of `region`. A program takes and returns all parts, laid end to end along the dimension named above; each array names one. Nothing has to cross between parts.
Inputs may be any that keep to these rules, and one draw needn't show every extreme that they name: `nearby_readings`: row c lists 128 distinct observations whose region-wide index o lies within (subarea_cutoff_level[c] + 2) * 64 of c and inside the region.
All inputs are finite; a program needn't handle non-finite values. Where the computation divides by a largest or mean magnitude, that divisor is 1e-20 or more.
Results may differ from a plain program's by a relative error of at most 0.0053.
Values may be sent and summed in bfloat16 or wider, within the bound.
A program may use at most 64 MiB of HBM per device.

v0:
```python
import functools

import jax
import jax.numpy as jnp
from jax import lax
from jax.experimental import pallas as pl
from jax.experimental.pallas import tpu as pltpu
from jax.sharding import PartitionSpec as P

NS_STEPS = 4
LANES = 128
GROUP = 4
CHUNK = 16
MESH = pl.DeviceIdType.MESH
F32 = jnp.float32
BF16 = jnp.bfloat16


def partner(me, k, n):
    if n & (n - 1):
        return lax.rem(me + k, n)
    other, bit = me, 1
    while bit < n:
        if k & bit:
            other = other + bit * (1 - 2 * lax.rem(me // bit, 2))
        bit *= 2
    return other


def split(value):
    high = value.astype(BF16)
    return high, (value - high.astype(F32)).astype(BF16)


def times(left, right):
    lh, ll = split(left)
    rh, rl = split(right)
    rows, k = left.shape[0], right.shape[0]
    lhs = jnp.concatenate([lh, ll], axis=0)[:, :k]
    rhs = jnp.concatenate([rh, rl], axis=1)
    out = jnp.dot(lhs, rhs, preferred_element_type=F32)
    width = right.shape[1]
    return out[:rows, :width] + out[:rows, width:] + out[rows:, :width]


def analyse_kernel(
    n, spaces, halo, obs_count, x, sensors_in, readings_in, noises_in, lists_in, tiers_in,
    out,
    sensors, readings, noises, lists, tiers, small_sem, pack, incoming, updated, gathered, full, anoms, anoms_t, marks, weights, gram, target, trans,
    moved, sums,
    in_send, in_recv, out_send, out_recv, local_sem, side_send, side_recv, sum_send, sum_recv,
):
    me = lax.axis_index("member")
    space = lax.axis_index("space")
    members, patch, _ = x.shape
    domains = patch // n
    lines = members * n
    width = anoms.shape[1]
    chunks = domains // CHUNK
    peers = n * spaces

    small = [
        pltpu.make_async_copy(source, place, small_sem.at[i])
        for i, (source, place) in enumerate(
            [
                (sensors_in, sensors), (readings_in, readings), (noises_in, noises),
                (lists_in.at[pl.ds(pl.multiple_of(me * domains, 8), domains)], lists),
                (tiers_in, tiers),
            ]
        )
    ]
    for copy in small:
        copy.start()

    def peer(k):
        other = lax.rem(me + space * n + k, peers)
        return {"member": lax.rem(other, n), "space": other // n}

    barrier = pltpu.get_barrier_semaphore()

    def greet(k, carry):
        pl.semaphore_signal(barrier, inc=1, device_id=peer(k), device_id_type=MESH)
        return carry

    lax.fori_loop(1, peers, greet, 0)
    for copy in small:
        copy.wait()
    rows = pack.shape[0]
    pack[...] = jnp.concatenate(
        [
            sensors[...].astype(F32), readings[...].astype(F32)[None],
            noises[...].astype(F32)[None], jnp.ones((rows - members - 2, patch), F32),
        ],
        axis=0,
    ).astype(BF16)
    gathered[1, me] = pack[...]

    lane = lax.broadcasted_iota(jnp.int32, (obs_count, width), 1)

    def mark(group, carry):
        start = pl.multiple_of(group * 8, 8)
        columns = jnp.transpose(lists[pl.ds(start, 8), :] - me * domains)
        found = []
        for d in range(8):
            hit = columns[:, d : d + 1] == lane
            found.append(jnp.sum(jnp.where(hit, 1.0, 0.0), axis=0, keepdims=True))
        marks[pl.ds(start, 8), :] = jnp.concatenate(found, axis=0)
        return carry

    pl.semaphore_wait(barrier, peers - 1)

    def side_copy(side, k):
        to_space = lax.rem(space + 1 - side + spaces, spaces)
        return pltpu.make_async_remote_copy(
            pack, gathered.at[side, me], side_send.at[side, k], side_recv.at[side, k],
            device_id={"member": partner(me, k, n), "space": to_space}, device_id_type=MESH,
        )

    has_left, has_right = space > 0, space < spaces - 1
    for k in range(1, n):
        side_copy(1, k).start()

    @pl.when(has_right)
    def _():
        for k in range(n):
            side_copy(0, k).start()

    @pl.when(has_left)
    def _():
        for k in range(n):
            side_copy(2, k).start()

    def in_views(to, g):
        return (
            x.at[:, pl.ds(pl.multiple_of(to * domains + g * CHUNK, 16), CHUNK), :],
            incoming.at[pl.ds(me * members, members), pl.ds(g * CHUNK, CHUNK), :],
        )

    def in_copy(g, k):
        to = partner(me, k, n)
        source, place = in_views(to, g)
        return pltpu.make_async_remote_copy(
            source, place, in_send.at[g, k], in_recv.at[g, k],
            device_id={"member": to}, device_id_type=MESH,
        )

    far_first = list(range(n // 2, n)) + list(range(1, n // 2))
    pairs = [(g, k) for g in range(chunks) for k in far_first]
    early = n - 1
    for g, k in pairs[:early]:
        in_copy(g, k).start()
    own = []
    for g in range(chunks):
        source, place = in_views(me, g)
        copy = pltpu.make_async_copy(source, place, local_sem.at[0, g])
        copy.start()
        own.append(copy)

    @pl.when(space == 0)
    def _():
        gathered[0] = jnp.ones(gathered.shape[1:], BF16)

    @pl.when(space == spaces - 1)
    def _():
        gathered[2] = jnp.ones(gathered.shape[1:], BF16)

    lax.fori_loop(0, domains // 8, mark, 0)

    for k in range(1, n):
        side_copy(1, k).wait()

    @pl.when(has_right)
    def _():
        for k in range(n):
            side_copy(0, k).wait_send()
            side_copy(2, k).wait_recv()

    @pl.when(has_left)
    def _():
        for k in range(n):
            side_copy(2, k).wait_send()
            side_copy(0, k).wait_recv()

    for side in range(3):
        for s in range(n):
            full[members * s : members * (s + 1), patch * side : patch * (side + 1)] = (
                gathered[side, s, :members, :].astype(F32)
            )
        full[lines : lines + 2, patch * side : patch * (side + 1)] = (
            gathered[side, 0, members : members + 2, :].astype(F32)
        )
    total = 3 * patch
    shift = lax.rem(2 * total - (patch - halo) - me * domains, total)
    turned = pltpu.roll(full[...], shift, 1)[:, :width]
    values = turned[:lines]
    mean = jnp.sum(values, axis=0, keepdims=True) * (1.0 / lines)
    anomaly = values - mean
    anoms[...] = anomaly
    innov = turned[lines : lines + 1] - mean
    noise = turned[lines + 1 : lines + 2]
    squares = jnp.sum(anomaly * anomaly, axis=0, keepdims=True)

    own_tier = lax.broadcasted_iota(jnp.int32, (domains, patch), 1) == (
        lax.broadcasted_iota(jnp.int32, (domains, patch), 0) + me * domains
    )
    tier = jnp.sum(jnp.where(own_tier, tiers[...].astype(F32)[None], 0.0), axis=1, keepdims=True)
    radius = (tier + 2.0) * (0.5 * obs_count)
    place = lax.broadcasted_iota(jnp.int32, (domains, width), 1)
    row = lax.broadcasted_iota(jnp.int32, (domains, width), 0)
    distance = jnp.abs(place - halo - row).astype(F32) / radius
    weight = marks[...] * jnp.exp(-2.0 * distance * distance) / noise
    weights[...] = weight
    fit = jnp.sum(weight * (innov * innov))
    spread = jnp.sum(weight * squares)
    first = lax.broadcasted_iota(jnp.int32, (1, LANES), 1) == 0
    moved[...] = jnp.where(first, fit, spread)

    high, low = split(anomaly)
    pad = jnp.zeros((LANES - lines, width), F32)
    anoms_t[...] = jnp.concatenate(
        [
            jnp.transpose(jnp.concatenate([high.astype(F32), pad], axis=0)),
            jnp.transpose(jnp.concatenate([low.astype(F32), pad], axis=0)),
        ],
        axis=1,
    ).astype(BF16)

    def sum_copy(k):
        return pltpu.make_async_remote_copy(
            moved, sums.at[k], sum_send.at[k], sum_recv.at[k],
            device_id=peer(k), device_id_type=MESH,
        )

    def start_sum(k, carry):
        sum_copy(k).start()
        return carry

    def end_sum(k, carry):
        sum_copy(k).wait()
        return carry + sums[k]

    lax.fori_loop(1, peers, start_sum, 0)
    for g, k in pairs[early:]:
        in_copy(g, k).start()

    hi, lo = split(weight * innov)
    aims = jnp.dot(jnp.concatenate([hi, lo], axis=0), anoms_t[...], preferred_element_type=F32)
    target[...] = aims[:domains, :LANES] + aims[:domains, LANES:] + aims[domains:, :LANES]

    def gram_group(g, carry):
        for d in range(2):
            c = g * 2 + d
            hi, lo = split(anoms[...] * weights[pl.ds(c, 1), :])
            prod = jnp.dot(
                jnp.concatenate([hi, lo], axis=0), anoms_t[...], preferred_element_type=F32
            )
            gram[c] = prod[:lines, :LANES] + prod[:lines, LANES:] + prod[lines:, :LANES]
        return carry

    lax.fori_loop(0, domains // 2, gram_group, 0)

    sums_all = lax.fori_loop(1, peers, end_sum, moved[...])
    scale = sums_all[:, 1:2] / sums_all[:, 0:1]
    eye = jnp.where(
        lax.broadcasted_iota(jnp.int32, (lines, LANES), 0)
        == lax.broadcasted_iota(jnp.int32, (lines, LANES), 1),
        1.0, 0.0,
    )
    diagonal = eye * scale

    def solve_group(g, carry):
        ids = [g * GROUP + d for d in range(GROUP)]
        mats = [gram[c] + diagonal for c in ids]
        bounds = [
            jnp.max(jnp.sum(jnp.abs(m), axis=0, keepdims=True), axis=1, keepdims=True)
            for m in mats
        ]
        ys = [m / b for m, b in zip(mats, bounds)]
        zs = [1.5 * eye - 0.5 * y for y in ys]
        ys = [times(y, z) for y, z in zip(ys, zs)]
        for step in range(1, NS_STEPS):
            ps = [1.5 * eye - 0.5 * times(z, y) for z, y in zip(zs, ys)]
            if step < NS_STEPS - 1:
                both = [
                    times(jnp.concatenate([y, z], axis=0), p) for y, z, p in zip(ys, zs, ps)
                ]
                ys = [b[:lines] for b in both]
                zs = [b[lines:] for b in both]
            else:
                zs = [times(z, p) for z, p in zip(zs, ps)]
        roots = [z * lax.rsqrt(b) for z, b in zip(zs, bounds)]
        for c, root in zip(ids, roots):
            half_gain = jnp.sum(root * target[pl.ds(c, 1), :], axis=1, keepdims=True)
            gain = jnp.sum(root * half_gain, axis=0, keepdims=True)
            w = (lines - 1.0) ** 0.5 * root + gain
            w = w - jnp.sum(w, axis=1, keepdims=True) * (1.0 / lines) + 1.0 / lines
            trans[c] = w.astype(BF16)
        return carry

    def out_views(to, g):
        return (
            updated.at[pl.ds(to * members, members), pl.ds(g * CHUNK, CHUNK), :],
            out.at[:, pl.ds(pl.multiple_of(me * domains + g * CHUNK, 16), CHUNK), :],
        )

    def out_copy(g, k):
        to = partner(me, k, n)
        source, place = out_views(to, g)
        return pltpu.make_async_remote_copy(
            source, place, out_send.at[g, k], out_recv.at[g, k],
            device_id={"member": to}, device_id_type=MESH,
        )

    for g in range(chunks):
        lax.fori_loop(g * CHUNK // GROUP, (g + 1) * CHUNK // GROUP, solve_group, 0)
        own[g].wait()
        for k in range(1, n):
            in_copy(g, k).wait()
        states = jnp.swapaxes(incoming[:, g * CHUNK : (g + 1) * CHUNK, :].astype(F32), 0, 1)
        states = states.astype(BF16)
        results = [
            jnp.dot(trans[g * CHUNK + c][:, :lines], states[c], preferred_element_type=F32)
            for c in range(CHUNK)
        ]
        results = jnp.stack(results, axis=0)
        updated[:, g * CHUNK : (g + 1) * CHUNK, :] = jnp.swapaxes(results, 0, 1).astype(BF16)
        for k in far_first:
            out_copy(g, k).start()
        source, place = out_views(me, g)
        copy = pltpu.make_async_copy(source, place, local_sem.at[1, g])
        copy.start()
        own.append(copy)

    for g in range(chunks):
        own[chunks + g].wait()
        for k in range(1, n):
            out_copy(g, k).wait()


def per_device(trials, sensors, readings, noises, lists, tiers):
    n, spaces = lax.axis_size("member"), lax.axis_size("space")
    members, patch, quantities = trials.shape
    obs_count = lists.shape[1]
    halo = 5 * obs_count // 2
    domains = patch // n
    chunks = domains // CHUNK
    lines = members * n
    width = -(-(domains + 2 * halo) // 256) * 256
    rows = -(-(members + 2) // 16) * 16
    vmem = pl.BlockSpec(memory_space=pltpu.VMEM)
    anywhere = pl.BlockSpec(memory_space=pl.ANY)
    full_rows = -(-(lines + 2) // 8) * 8
    dma = pltpu.SemaphoreType.DMA
    return pl.pallas_call(
        functools.partial(analyse_kernel, n, spaces, halo, obs_count),
        out_shape=jax.ShapeDtypeStruct((members, patch, quantities), BF16),
        in_specs=[anywhere] * 6,
        out_specs=vmem,
        scratch_shapes=[
            pltpu.VMEM((members, patch), BF16),
            pltpu.VMEM((patch,), BF16),
            pltpu.VMEM((patch,), BF16),
            pltpu.VMEM((domains, obs_count), jnp.int32),
            pltpu.VMEM((patch,), jnp.int32),
            dma((5,)),
            pltpu.VMEM((rows, patch), BF16),
            pltpu.VMEM((lines, domains, quantities), BF16),
            pltpu.VMEM((lines, domains, quantities), BF16),
            pltpu.VMEM((3, n, rows, patch), BF16),
            pltpu.VMEM((full_rows, 3 * patch), F32),
            pltpu.VMEM((lines, width), F32),
            pltpu.VMEM((width, 2 * LANES), BF16),
            pltpu.VMEM((domains, width), F32),
            pltpu.VMEM((domains, width), F32),
            pltpu.VMEM((domains, lines, LANES), F32),
            pltpu.VMEM((domains, LANES), F32),
            pltpu.VMEM((domains, lines, LANES), BF16),
            pltpu.VMEM((1, LANES), F32),
            pltpu.VMEM((n * spaces, 1, LANES), F32),
            dma((chunks, n)), dma((chunks, n)), dma((chunks, n)), dma((chunks, n)),
            dma((2, chunks)), dma((3, n)), dma((3, n)), dma((n * spaces,)), dma((n * spaces,)),
        ],
        compiler_params=pltpu.CompilerParams(
            collective_id=0, has_side_effects=True, vmem_limit_bytes=63 << 20
        ),
        name="analyse",
    )(trials, sensors, readings, noises, lists, tiers)


def solution(mesh):
    return jax.shard_map(
        per_device,
        mesh=mesh,
        in_specs=(
            P("member", ("region", "space"), None),
            P("member", ("region", "space")),
            P(("region", "space")),
            P(("region", "space")),
            P(("region", "space"), None),
            P(("region", "space")),
        ),
        out_specs=P("member", ("region", "space"), None),
        check_vma=False,
    )
```

profile of v0, /device:TPU:10, one launch (start us, length us, event | category | flops | bytes accessed | tf_op | source)
XLA Modules:
  0.0 98.8 jit_solution(4964024268876777816)
XLA Ops:
  0.0 95.8 %analyse.1 = bf16[10,384,256]{2,1,0:T(8,128)(2,1)} custom-call(bf16[10,384,256]{2,1,0:T(8,128)(2,1)} %x.1, bf16[10,384]{1,0:T(8,128)(2,1)} %sensors_in.1, bf16[384]{0:T(512)(128)(2,1)} %readings_in.1, bf16[384]{0:T(512)(128)(2,1)} %noises_in.1, s32[384,128]{1,0:T(8,128)} %lists_in.1, s32[384]{0:T(512)} %tiers_in.1), custom_call_target="tpu_custom_call" | custom-call | tf_op jit(solution)/shard_map/analyse/pallas_call | solution.py:354
  95.8 2.9 %copy.8 = bf16[10,384,256]{2,1,0:T(8,128)(2,1)} copy(bf16[10,384,256]{2,1,0:T(8,128)(2,1)} %analyse.1) | data formatting | bytes 3932160
where the time goes:
time: 100 us; the launch traced here: 98.8 us
  Pallas kernels  95.8 us (96%)
  local copies, waits for them, and re-layouts  2.94 us (3%)
    pallas_call x1, Pallas kernels, per_device(): pl.pallas_call(functools.partial(analyse_kernel, n, spaces, halo, obs_cou...  95.8 us
    unnamed x1, local copies, waits for them, and re-layouts  2.94 us

commit v1 on v0

--- a/solution.py
+++ b/solution.py
@@ -348,12 +348,12 @@
     width = -(-(domains + 2 * halo) // 256) * 256
     rows = -(-(members + 2) // 16) * 16
     vmem = pl.BlockSpec(memory_space=pltpu.VMEM)
-    anywhere = pl.BlockSpec(memory_space=pl.ANY)
+    anywhere = pl.BlockSpec(memory_space=pltpu.HBM)
     full_rows = -(-(lines + 2) // 8) * 8
     dma = pltpu.SemaphoreType.DMA
     return pl.pallas_call(
         functools.partial(analyse_kernel, n, spaces, halo, obs_count),
-        out_shape=jax.ShapeDtypeStruct((members, patch, quantities), BF16),
+        out_shape=pltpu.VMEM((members, patch, quantities), BF16),
         in_specs=[anywhere] * 6,
         out_specs=vmem,
         scratch_shapes=[
@@ -381,10 +381,10 @@
             dma((2, chunks)), dma((3, n)), dma((3, n)), dma((n * spaces,)), dma((n * spaces,)),
         ],
         compiler_params=pltpu.CompilerParams(
-            collective_id=0, has_side_effects=True, vmem_limit_bytes=63 << 20
+            collective_id=0, has_side_effects=True, vmem_limit_bytes=40 << 20
         ),
         name="analyse",
-    )(trials, sensors, readings, noises, lists, tiers)
+    )(*[pltpu.with_memory_space_constraint(a, pltpu.HBM) for a in (trials, sensors, readings, noises, lists, tiers)])
 
 
 def solution(mesh):

time: 100 us -> 97 us (0.970)
  local copies, waits for them, and re-layouts: 2.94 us -> 1.27 us
  Pallas kernels: 95.8 us -> 94.5 us
    unnamed x1, local copies, waits for them, and re-layouts: 2.94 us -> 1.27 us
    pallas_call x1, Pallas kernels: 95.8 us -> 94.5 us  [per_device(): pl.pallas_call(functools.partial(analyse_kernel, n, spaces, halo, obs_cou...]
where the time goes in v1:
time: 97 us; the launch traced here: 95.8 us
  Pallas kernels  94.5 us (97%)
  local copies, waits for them, and re-layouts  1.27 us (1%)
    pallas_call x1, Pallas kernels, per_device(): pl.pallas_call(functools.partial(analyse_kernel, n, spaces, halo, obs_cou...  94.5 us

profile of v1, /device:TPU:10, one launch (start us, length us, event | category | flops | bytes accessed | tf_op | source)
XLA Modules:
  0.0 95.8 jit_solution(7997477212494993290)
XLA Ops:
  0.0 94.5 %analyse.1 = bf16[10,384,256]{2,1,0:T(8,128)(2,1)S(1)} custom-call(bf16[10,384,256]{2,1,0:T(8,128)(2,1)} %x.1, bf16[10,384]{1,0:T(8,128)(2,1)} %sensors_in.1, bf16[384]{0:T(512)(128)(2,1)} %readings_in.1, bf16[384]{0:T(512)(128)(2,1)} %noises_in.1, s32[384,128]{1,0:T(8,128)} %lists_in.1, s32[384]{0:T(512)} %tiers_in.1), custom_call_target="tpu_custom_call" | custom-call | tf_op jit(solution)/shard_map/analyse/pallas_call | solution.py:354
  94.5 1.3 %copy.8 = bf16[10,384,256]{2,1,0:T(8,128)(2,1)} copy(bf16[10,384,256]{2,1,0:T(8,128)(2,1)S(1)} %analyse.1) | data formatting | bytes 3932160

commit v2 on v1

--- a/solution.py
+++ b/solution.py
@@ -46,9 +46,9 @@
 def analyse_kernel(
     n, spaces, halo, obs_count, x, sensors_in, readings_in, noises_in, lists_in, tiers_in,
     out,
-    sensors, readings, noises, lists, tiers, small_sem, pack, incoming, updated, gathered, full, anoms, anoms_t, marks, weights, gram, target, trans,
+    readings, noises, left_readings, left_noises, right_readings, right_noises, lists, tiers, small_sem, incoming, updated, gathered, full, anoms, anoms_t, marks, weights, gram, target, trans,
     moved, sums,
-    in_send, in_recv, out_send, out_recv, local_sem, side_send, side_recv, sum_send, sum_recv,
+    in_send, in_recv, out_send, out_recv, local_sem, near_send, near_recv, chip_send, chip_recv, side_send, side_recv, sum_send, sum_recv,
 ):
     me = lax.axis_index("member")
     space = lax.axis_index("space")
@@ -58,12 +58,18 @@
     width = anoms.shape[1]
     chunks = domains // CHUNK
     peers = n * spaces
+    cores = 2 - n % 2
+    chips = n // cores
+    core, chip = lax.rem(me, cores), me // cores
+
+    def slot(member):
+        return lax.rem(member, cores) * chips + member // cores
 
     small = [
         pltpu.make_async_copy(source, place, small_sem.at[i])
         for i, (source, place) in enumerate(
             [
-                (sensors_in, sensors), (readings_in, readings), (noises_in, noises),
+                (sensors_in, gathered.at[1, slot(me)]), (readings_in, readings), (noises_in, noises),
                 (lists_in.at[pl.ds(pl.multiple_of(me * domains, 8), domains)], lists),
                 (tiers_in, tiers),
             ]
@@ -83,17 +89,7 @@
         return carry
 
     lax.fori_loop(1, peers, greet, 0)
-    for copy in small:
-        copy.wait()
-    rows = pack.shape[0]
-    pack[...] = jnp.concatenate(
-        [
-            sensors[...].astype(F32), readings[...].astype(F32)[None],
-            noises[...].astype(F32)[None], jnp.ones((rows - members - 2, patch), F32),
-        ],
-        axis=0,
-    ).astype(BF16)
-    gathered[1, me] = pack[...]
+    small[0].wait()
 
     lane = lax.broadcasted_iota(jnp.int32, (obs_count, width), 1)
 
@@ -107,28 +103,55 @@
         marks[pl.ds(start, 8), :] = jnp.concatenate(found, axis=0)
         return carry
 
-    pl.semaphore_wait(barrier, peers - 1)
-
-    def side_copy(side, k):
-        to_space = lax.rem(space + 1 - side + spaces, spaces)
+    with jax.named_scope("w_barrier"):
+        pl.semaphore_wait(barrier, peers - 1)
+
+    has_left, has_right = space > 0, space < spaces - 1
+
+    def to_space(side):
+        return lax.rem(space + 1 - side + spaces, spaces)
+
+    def chip_copy(j):
+        place = gathered.at[1, slot(me)]
+        other = partner(chip, j, chips) * cores + core
         return pltpu.make_async_remote_copy(
-            pack, gathered.at[side, me], side_send.at[side, k], side_recv.at[side, k],
-            device_id={"member": partner(me, k, n), "space": to_space}, device_id_type=MESH,
-        )
-
-    has_left, has_right = space > 0, space < spaces - 1
-    for k in range(1, n):
-        side_copy(1, k).start()
+            place, place, chip_send.at[j], chip_recv.at[j],
+            device_id={"member": other}, device_id_type=MESH,
+        )
+
+    singles = [(left_readings, left_noises), (readings, noises), (right_readings, right_noises)]
+
+    def near_copies(side):
+        index = side // 2
+        return [
+            pltpu.make_async_remote_copy(
+                source, place, near_send.at[index, i], near_recv.at[index, i],
+                device_id={"space": to_space(side)}, device_id_type=MESH,
+            )
+            for i, (source, place) in enumerate(zip((readings_in, noises_in), singles[side]))
+        ]
+
+    def side_copy(side, t):
+        rows = pl.ds(core * chips, chips)
+        return pltpu.make_async_remote_copy(
+            gathered.at[1, rows], gathered.at[side, rows],
+            side_send.at[side, t], side_recv.at[side, t],
+            device_id={"member": chip * cores + lax.rem(core + t, cores), "space": to_space(side)},
+            device_id_type=MESH,
+        )
+
+    for j in range(1, chips):
+        chip_copy(j).start()
 
     @pl.when(has_right)
     def _():
-        for k in range(n):
-            side_copy(0, k).start()
+        for copy in near_copies(0):
+            copy.start()
 
     @pl.when(has_left)
     def _():
-        for k in range(n):
-            side_copy(2, k).start()
+        for copy in near_copies(2):
+            copy.start()
 
     def in_views(to, g):
         return (
@@ -144,11 +167,24 @@
             device_id={"member": to}, device_id_type=MESH,
         )
 
-    far_first = list(range(n // 2, n)) + list(range(1, n // 2))
+    far = list(range(n // 2, n))
+    close = list(range(1, n // 2))
+    far_first = far + close
+    middle = (me >= n // 2 - cores) & (me < n // 2 + cores)
     pairs = [(g, k) for g in range(chunks) for k in far_first]
-    early = n - 1
-    for g, k in pairs[:early]:
-        in_copy(g, k).start()
+    middle_early = [(0, k) for k in far_first]
+    outer_early = [(g, k) for g in range(chunks) for k in close]
+
+    @pl.when(middle)
+    def _():
+        for g, k in middle_early:
+            in_copy(g, k).start()
+
+    @pl.when(jnp.logical_not(middle))
+    def _():
+        for g, k in outer_early:
+            in_copy(g, k).start()
+
     own = []
     for g in range(chunks):
         source, place = in_views(me, g)
@@ -156,39 +192,68 @@
         copy.start()
         own.append(copy)
 
-    @pl.when(space == 0)
-    def _():
-        gathered[0] = jnp.ones(gathered.shape[1:], BF16)
-
-    @pl.when(space == spaces - 1)
-    def _():
-        gathered[2] = jnp.ones(gathered.shape[1:], BF16)
-
-    lax.fori_loop(0, domains // 8, mark, 0)
-
-    for k in range(1, n):
-        side_copy(1, k).wait()
+    for side, missing in ((0, space == 0), (2, space == spaces - 1)):
+        @pl.when(missing)
+        def _():
+            gathered[side] = jnp.ones(gathered.shape[1:], BF16)
+            for single in singles[side]:
+                single[...] = jnp.ones(single.shape, BF16)
+
+    for copy in small[1:]:
+        copy.wait()
+    with jax.named_scope("marks"):
+        lax.fori_loop(0, domains // 8, mark, 0)
+
+    with jax.named_scope("w_chip"):
+        for j in range(1, chips):
+            chip_copy(j).wait()
+
+    for t in range(1, cores):
+        side_copy(1, t).start()
 
     @pl.when(has_right)
     def _():
-        for k in range(n):
-            side_copy(0, k).wait_send()
-            side_copy(2, k).wait_recv()
+        for t in range(cores):
+            side_copy(0, t).start()
 
     @pl.when(has_left)
     def _():
-        for k in range(n):
-            side_copy(2, k).wait_send()
-            side_copy(0, k).wait_recv()
+        for t in range(cores):
+            side_copy(2, t).start()
+
+    with jax.named_scope("w_side"):
+        for t in range(1, cores):
+            side_copy(1, t).wait()
+
+        @pl.when(has_right)
+        def _():
+            for copy in near_copies(0):
+                copy.wait_send()
+            for copy in near_copies(2):
+                copy.wait_recv()
+            for t in range(cores):
+                side_copy(0, t).wait_send()
+                side_copy(2, t).wait_recv()
+
+        @pl.when(has_left)
+        def _():
+            for copy in near_copies(2):
+                copy.wait_send()
+            for copy in near_copies(0):
+                copy.wait_recv()
+            for t in range(cores):
+                side_copy(2, t).wait_send()
+                side_copy(0, t).wait_recv()
 
     for side in range(3):
         for s in range(n):
             full[members * s : members * (s + 1), patch * side : patch * (side + 1)] = (
-                gathered[side, s, :members, :].astype(F32)
+                gathered[side, s % cores * chips + s // cores].astype(F32)
             )
-        full[lines : lines + 2, patch * side : patch * (side + 1)] = (
-            gathered[side, 0, members : members + 2, :].astype(F32)
-        )
+        for i, single in enumerate(singles[side]):
+            full[lines + i : lines + i + 1, patch * side : patch * (side + 1)] = (
+                single[...].astype(F32)[None]
+            )
     total = 3 * patch
     shift = lax.rem(2 * total - (patch - halo) - me * domains, total)
     turned = pltpu.roll(full[...], shift, 1)[:, :width]
@@ -240,8 +305,12 @@
         return carry + sums[k]
 
     lax.fori_loop(1, peers, start_sum, 0)
-    for g, k in pairs[early:]:
-        in_copy(g, k).start()
+
+    @pl.when(middle)
+    def _():
+        for g, k in pairs:
+            if (g, k) not in middle_early:
+                in_copy(g, k).start()
 
     hi, lo = split(weight * innov)
     aims = jnp.dot(jnp.concatenate([hi, lo], axis=0), anoms_t[...], preferred_element_type=F32)
@@ -257,9 +326,18 @@
             gram[c] = prod[:lines, :LANES] + prod[:lines, LANES:] + prod[lines:, :LANES]
         return carry
 
-    lax.fori_loop(0, domains // 2, gram_group, 0)
-
-    sums_all = lax.fori_loop(1, peers, end_sum, moved[...])
+    with jax.named_scope('gram'):
+        lax.fori_loop(0, domains // 2, gram_group, 0)
+
+    with jax.named_scope("w_sums"):
+        sums_all = lax.fori_loop(1, peers, end_sum, moved[...])
+
+    @pl.when(jnp.logical_not(middle))
+    def _():
+        for g, k in pairs:
+            if (g, k) not in outer_early:
+                in_copy(g, k).start()
+
     scale = sums_all[:, 1:2] / sums_all[:, 0:1]
     eye = jnp.where(
         lax.broadcasted_iota(jnp.int32, (lines, LANES), 0)
@@ -312,10 +390,12 @@
         )
 
     for g in range(chunks):
-        lax.fori_loop(g * CHUNK // GROUP, (g + 1) * CHUNK // GROUP, solve_group, 0)
-        own[g].wait()
-        for k in range(1, n):
-            in_copy(g, k).wait()
+        with jax.named_scope(f'solve{g}'):
+            lax.fori_loop(g * CHUNK // GROUP, (g + 1) * CHUNK // GROUP, solve_group, 0)
+        with jax.named_scope(f'w_in{g}'):
+            own[g].wait()
+            for k in range(1, n):
+                in_copy(g, k).wait()
         states = jnp.swapaxes(incoming[:, g * CHUNK : (g + 1) * CHUNK, :].astype(F32), 0, 1)
         states = states.astype(BF16)
         results = [
@@ -332,9 +412,10 @@
         own.append(copy)
 
     for g in range(chunks):
-        own[chunks + g].wait()
-        for k in range(1, n):
-            out_copy(g, k).wait()
+        with jax.named_scope(f'w_out{g}'):
+            own[chunks + g].wait()
+            for k in range(1, n):
+                out_copy(g, k).wait()
 
 
 def per_device(trials, sensors, readings, noises, lists, tiers):
@@ -346,7 +427,6 @@
     chunks = domains // CHUNK
     lines = members * n
     width = -(-(domains + 2 * halo) // 256) * 256
-    rows = -(-(members + 2) // 16) * 16
     vmem = pl.BlockSpec(memory_space=pltpu.VMEM)
     anywhere = pl.BlockSpec(memory_space=pltpu.HBM)
     full_rows = -(-(lines + 2) // 8) * 8
@@ -357,16 +437,18 @@
         in_specs=[anywhere] * 6,
         out_specs=vmem,
         scratch_shapes=[
-            pltpu.VMEM((members, patch), BF16),
+            pltpu.VMEM((patch,), BF16),
+            pltpu.VMEM((patch,), BF16),
+            pltpu.VMEM((patch,), BF16),
+            pltpu.VMEM((patch,), BF16),
             pltpu.VMEM((patch,), BF16),
             pltpu.VMEM((patch,), BF16),
             pltpu.VMEM((domains, obs_count), jnp.int32),
             pltpu.VMEM((patch,), jnp.int32),
             dma((5,)),
-            pltpu.VMEM((rows, patch), BF16),
             pltpu.VMEM((lines, domains, quantities), BF16),
             pltpu.VMEM((lines, domains, quantities), BF16),
-            pltpu.VMEM((3, n, rows, patch), BF16),
+            pltpu.VMEM((3, n, members, patch), BF16),
             pltpu.VMEM((full_rows, 3 * patch), F32),
             pltpu.VMEM((lines, width), F32),
             pltpu.VMEM((width, 2 * LANES), BF16),
@@ -378,7 +460,8 @@
             pltpu.VMEM((1, LANES), F32),
             pltpu.VMEM((n * spaces, 1, LANES), F32),
             dma((chunks, n)), dma((chunks, n)), dma((chunks, n)), dma((chunks, n)),
-            dma((2, chunks)), dma((3, n)), dma((3, n)), dma((n * spaces,)), dma((n * spaces,)),
+            dma((2, chunks)), dma((2, 2)), dma((2, 2)), dma((n,)), dma((n,)), dma((3, 2)), dma((3, 2)),
+            dma((n * spaces,)), dma((n * spaces,)),
         ],
         compiler_params=pltpu.CompilerParams(
             collective_id=0, has_side_effects=True, vmem_limit_bytes=40 << 20

time: 97 us -> 94.6 us (0.975)
  Pallas kernels: 94.5 us -> 92.7 us
    pallas_call x1, Pallas kernels: 94.5 us -> 92.7 us  [per_device(): pl.pallas_call(functools.partial(analyse_kernel, n, spaces, halo, obs_cou...]
where the time goes in v2:
time: 94.6 us; the launch traced here: 94 us
  Pallas kernels  92.7 us (98%)
  local copies, waits for them, and re-layouts  1.27 us (1%)
    pallas_call x1, Pallas kernels, per_device(): pl.pallas_call(functools.partial(analyse_kernel, n, spaces, halo, obs_cou...  92.7 us

profile of v2, /device:TPU:10, one launch (start us, length us, event | category | flops | bytes accessed | tf_op | source)
XLA Modules:
  0.0 94.0 jit_solution(11628522652230662877)
XLA Ops:
  0.0 92.7 %analyse.1 = bf16[10,384,256]{2,1,0:T(8,128)(2,1)S(1)} custom-call(bf16[10,384,256]{2,1,0:T(8,128)(2,1)} %x.1, bf16[10,384]{1,0:T(8,128)(2,1)} %sensors_in.1, bf16[384]{0:T(512)(128)(2,1)} %readings_in.1, bf16[384]{0:T(512)(128)(2,1)} %noises_in.1, s32[384,128]{1,0:T(8,128)} %lists_in.1, s32[384]{0:T(512)} %tiers_in.1), custom_call_target="tpu_custom_call" | custom-call | tf_op jit(solution)/shard_map/analyse/pallas_call | solution.py:434
  92.7 1.3 %copy.8 = bf16[10,384,256]{2,1,0:T(8,128)(2,1)} copy(bf16[10,384,256]{2,1,0:T(8,128)(2,1)S(1)} %analyse.1) | data formatting | bytes 3932160

commit v3 on v2

--- a/solution.py
+++ b/solution.py
@@ -48,7 +48,7 @@
     out,
     readings, noises, left_readings, left_noises, right_readings, right_noises, lists, tiers, small_sem, incoming, updated, gathered, full, anoms, anoms_t, marks, weights, gram, target, trans,
     moved, sums,
-    in_send, in_recv, out_send, out_recv, local_sem, near_send, near_recv, chip_send, chip_recv, side_send, side_recv, sum_send, sum_recv,
+    in_send, in_recv, out_send, out_recv, near_send, near_recv, chip_send, chip_recv, side_send, side_recv, sum_send, sum_recv,
 ):
     me = lax.axis_index("member")
     space = lax.axis_index("space")
@@ -62,6 +62,9 @@
     chips = n // cores
     core, chip = lax.rem(me, cores), me // cores
 
+    def landed(ref, sem):
+        pltpu.make_async_copy(ref, ref, sem).wait()
+
     def slot(member):
         return lax.rem(member, cores) * chips + member // cores
 
@@ -115,7 +118,7 @@
         place = gathered.at[1, slot(me)]
         other = partner(chip, j, chips) * cores + core
         return pltpu.make_async_remote_copy(
-            place, place, chip_send.at[j], chip_recv.at[j],
+            place, place, chip_send.at[0], chip_recv.at[0],
             device_id={"member": other}, device_id_type=MESH,
         )
 
@@ -135,7 +138,7 @@
         rows = pl.ds(core * chips, chips)
         return pltpu.make_async_remote_copy(
             gathered.at[1, rows], gathered.at[side, rows],
-            side_send.at[side, t], side_recv.at[side, t],
+            side_send.at[side], side_recv.at[side],
             device_id={"member": chip * cores + lax.rem(core + t, cores), "space": to_space(side)},
             device_id_type=MESH,
         )
@@ -163,7 +166,7 @@
         to = partner(me, k, n)
         source, place = in_views(to, g)
         return pltpu.make_async_remote_copy(
-            source, place, in_send.at[g, k], in_recv.at[g, k],
+            source, place, in_send.at[0], in_recv.at[g],
             device_id={"member": to}, device_id_type=MESH,
         )
 
@@ -185,12 +188,9 @@
         for g, k in outer_early:
             in_copy(g, k).start()
 
-    own = []
     for g in range(chunks):
         source, place = in_views(me, g)
-        copy = pltpu.make_async_copy(source, place, local_sem.at[0, g])
-        copy.start()
-        own.append(copy)
+        pltpu.make_async_copy(source, place, in_recv.at[g]).start()
 
     for side, missing in ((0, space == 0), (2, space == spaces - 1)):
         @pl.when(missing)
@@ -205,8 +205,10 @@
         lax.fori_loop(0, domains // 8, mark, 0)
 
     with jax.named_scope("w_chip"):
-        for j in range(1, chips):
-            chip_copy(j).wait()
+        if chips > 1:
+            others = gathered.at[1, pl.ds(0, chips - 1)]
+            landed(others, chip_send.at[0])
+            landed(others, chip_recv.at[0])
 
     for t in range(1, cores):
         side_copy(1, t).start()
@@ -222,8 +224,10 @@
             side_copy(2, t).start()
 
     with jax.named_scope("w_side"):
-        for t in range(1, cores):
-            side_copy(1, t).wait()
+        if cores > 1:
+            others = gathered.at[1, pl.ds(0, n - chips)]
+            landed(others, side_send.at[1])
+            landed(others, side_recv.at[1])
 
         @pl.when(has_right)
         def _():
@@ -231,9 +235,8 @@
                 copy.wait_send()
             for copy in near_copies(2):
                 copy.wait_recv()
-            for t in range(cores):
-                side_copy(0, t).wait_send()
-                side_copy(2, t).wait_recv()
+            landed(gathered.at[1], side_send.at[0])
+            landed(gathered.at[2], side_recv.at[2])
 
         @pl.when(has_left)
         def _():
@@ -241,9 +244,8 @@
                 copy.wait_send()
             for copy in near_copies(0):
                 copy.wait_recv()
-            for t in range(cores):
-                side_copy(2, t).wait_send()
-                side_copy(0, t).wait_recv()
+            landed(gathered.at[1], side_send.at[2])
+            landed(gathered.at[0], side_recv.at[0])
 
     for side in range(3):
         for s in range(n):
@@ -292,7 +294,7 @@
 
     def sum_copy(k):
         return pltpu.make_async_remote_copy(
-            moved, sums.at[k], sum_send.at[k], sum_recv.at[k],
+            moved, sums.at[k], sum_send.at[0], sum_recv.at[0],
             device_id=peer(k), device_id_type=MESH,
         )
 
@@ -300,8 +302,7 @@
         sum_copy(k).start()
         return carry
 
-    def end_sum(k, carry):
-        sum_copy(k).wait()
+    def add_sum(k, carry):
         return carry + sums[k]
 
     lax.fori_loop(1, peers, start_sum, 0)
@@ -330,7 +331,11 @@
         lax.fori_loop(0, domains // 2, gram_group, 0)
 
     with jax.named_scope("w_sums"):
-        sums_all = lax.fori_loop(1, peers, end_sum, moved[...])
+        if peers > 1:
+            others = sums.at[pl.ds(1, peers - 1)]
+            landed(others, sum_send.at[0])
+            landed(others, sum_recv.at[0])
+        sums_all = lax.fori_loop(1, peers, add_sum, moved[...])
 
     @pl.when(jnp.logical_not(middle))
     def _():
@@ -385,7 +390,7 @@
         to = partner(me, k, n)
         source, place = out_views(to, g)
         return pltpu.make_async_remote_copy(
-            source, place, out_send.at[g, k], out_recv.at[g, k],
+            source, place, out_send.at[0], out_recv.at[0],
             device_id={"member": to}, device_id_type=MESH,
         )
 
@@ -393,9 +398,7 @@
         with jax.named_scope(f'solve{g}'):
             lax.fori_loop(g * CHUNK // GROUP, (g + 1) * CHUNK // GROUP, solve_group, 0)
         with jax.named_scope(f'w_in{g}'):
-            own[g].wait()
-            for k in range(1, n):
-                in_copy(g, k).wait()
+            landed(incoming.at[:, pl.ds(g * CHUNK, CHUNK), :], in_recv.at[g])
         states = jnp.swapaxes(incoming[:, g * CHUNK : (g + 1) * CHUNK, :].astype(F32), 0, 1)
         states = states.astype(BF16)
         results = [
@@ -407,15 +410,13 @@
         for k in far_first:
             out_copy(g, k).start()
         source, place = out_views(me, g)
-        copy = pltpu.make_async_copy(source, place, local_sem.at[1, g])
-        copy.start()
-        own.append(copy)
-
-    for g in range(chunks):
-        with jax.named_scope(f'w_out{g}'):
-            own[chunks + g].wait()
-            for k in range(1, n):
-                out_copy(g, k).wait()
+        pltpu.make_async_copy(source, place, out_recv.at[0]).start()
+
+    with jax.named_scope("w_out"):
+        if n > 1:
+            landed(x.at[:, pl.ds(0, patch - domains), :], in_send.at[0])
+            landed(updated.at[pl.ds(0, lines - members)], out_send.at[0])
+        landed(out, out_recv.at[0])
 
 
 def per_device(trials, sensors, readings, noises, lists, tiers):
@@ -459,9 +460,8 @@
             pltpu.VMEM((domains, lines, LANES), BF16),
             pltpu.VMEM((1, LANES), F32),
             pltpu.VMEM((n * spaces, 1, LANES), F32),
-            dma((chunks, n)), dma((chunks, n)), dma((chunks, n)), dma((chunks, n)),
-            dma((2, chunks)), dma((2, 2)), dma((2, 2)), dma((n,)), dma((n,)), dma((3, 2)), dma((3, 2)),
-            dma((n * spaces,)), dma((n * spaces,)),
+            dma((1,)), dma((chunks,)), dma((1,)), dma((1,)),
+            dma((2, 2)), dma((2, 2)), dma((1,)), dma((1,)), dma((3,)), dma((3,)), dma((1,)), dma((1,)),
         ],
         compiler_params=pltpu.CompilerParams(
             collective_id=0, has_side_effects=True, vmem_limit_bytes=40 << 20

time: 94.6 us -> 93.3 us (0.986)
  Pallas kernels: 92.7 us -> 91.4 us
    pallas_call x1, Pallas kernels: 92.7 us -> 91.4 us  [per_device(): pl.pallas_call(functools.partial(analyse_kernel, n, spaces, halo, obs_cou...]
where the time goes in v3:
time: 93.3 us; the launch traced here: 92.7 us
  Pallas kernels  91.4 us (98%)
  local copies, waits for them, and re-layouts  1.27 us (1%)
    pallas_call x1, Pallas kernels, per_device(): pl.pallas_call(functools.partial(analyse_kernel, n, spaces, halo, obs_cou...  91.4 us

profile of v3, /device:TPU:10, one launch (start us, length us, event | category | flops | bytes accessed | tf_op | source)
XLA Modules:
  0.0 92.7 jit_solution(12826892768647012219)
XLA Ops:
  0.0 91.4 %analyse.1 = bf16[10,384,256]{2,1,0:T(8,128)(2,1)S(1)} custom-call(bf16[10,384,256]{2,1,0:T(8,128)(2,1)} %x.1, bf16[10,384]{1,0:T(8,128)(2,1)} %sensors_in.1, bf16[384]{0:T(512)(128)(2,1)} %readings_in.1, bf16[384]{0:T(512)(128)(2,1)} %noises_in.1, s32[384,128]{1,0:T(8,128)} %lists_in.1, s32[384]{0:T(512)} %tiers_in.1), custom_call_target="tpu_custom_call" | custom-call | tf_op jit(solution)/shard_map/analyse/pallas_call | solution.py:435
  91.4 1.3 %copy.8 = bf16[10,384,256]{2,1,0:T(8,128)(2,1)} copy(bf16[10,384,256]{2,1,0:T(8,128)(2,1)S(1)} %analyse.1) | data formatting | bytes 3932160

commit v4 on v3

--- a/solution.py
+++ b/solution.py
@@ -46,7 +46,7 @@
 def analyse_kernel(
     n, spaces, halo, obs_count, x, sensors_in, readings_in, noises_in, lists_in, tiers_in,
     out,
-    readings, noises, left_readings, left_noises, right_readings, right_noises, lists, tiers, small_sem, incoming, updated, gathered, full, anoms, anoms_t, marks, weights, gram, target, trans,
+    entered, readings, noises, left_readings, left_noises, right_readings, right_noises, lists, tiers, small_sem, incoming, updated, gathered, full, anoms, anoms_t, marks, weights, gram, target, trans,
     moved, sums,
     in_send, in_recv, out_send, out_recv, near_send, near_recv, chip_send, chip_recv, side_send, side_recv, sum_send, sum_recv,
 ):
@@ -68,6 +68,27 @@
     def slot(member):
         return lax.rem(member, cores) * chips + member // cores
 
+    staged = n > 2 * cores and n & (n - 1) == 0
+    low = n // 2 - cores if staged else n
+    span = 2 * cores
+
+    def central(member):
+        return (member >= low) & (member < low + span)
+
+    middle = central(me)
+    outer = jnp.logical_not(middle)
+    barrier = pltpu.get_barrier_semaphore()
+
+    def peer(k):
+        other = lax.rem(me + space * n + k, peers)
+        return {"member": lax.rem(other, n), "space": other // n}
+
+    @pl.when(middle)
+    def _():
+        for k in range(1, span):
+            other = low + lax.rem(me - low + k, span)
+            pl.semaphore_signal(barrier, inc=1, device_id={"member": other}, device_id_type=MESH)
+
     small = [
         pltpu.make_async_copy(source, place, small_sem.at[i])
         for i, (source, place) in enumerate(
@@ -81,19 +102,16 @@
     for copy in small:
         copy.start()
 
-    def peer(k):
-        other = lax.rem(me + space * n + k, peers)
-        return {"member": lax.rem(other, n), "space": other // n}
-
-    barrier = pltpu.get_barrier_semaphore()
-
     def greet(k, carry):
-        pl.semaphore_signal(barrier, inc=1, device_id=peer(k), device_id_type=MESH)
+        other = peer(k)
+
+        @pl.when(jnp.logical_not(central(other["member"])))
+        def _():
+            pl.semaphore_signal(barrier, inc=1, device_id=other, device_id_type=MESH)
+
         return carry
 
     lax.fori_loop(1, peers, greet, 0)
-    small[0].wait()
-
     lane = lax.broadcasted_iota(jnp.int32, (obs_count, width), 1)
 
     def mark(group, carry):
@@ -106,8 +124,9 @@
         marks[pl.ds(start, 8), :] = jnp.concatenate(found, axis=0)
         return carry
 
-    with jax.named_scope("w_barrier"):
-        pl.semaphore_wait(barrier, peers - 1)
+    def marking(first, last):
+        with jax.named_scope("marks"):
+            lax.fori_loop(first, last, mark, 0)
 
     has_left, has_right = space > 0, space < spaces - 1
 
@@ -143,19 +162,6 @@
             device_id_type=MESH,
         )
 
-    for j in range(1, chips):
-        chip_copy(j).start()
-
-    @pl.when(has_right)
-    def _():
-        for copy in near_copies(0):
-            copy.start()
-
-    @pl.when(has_left)
-    def _():
-        for copy in near_copies(2):
-            copy.start()
-
     def in_views(to, g):
         return (
             x.at[:, pl.ds(pl.multiple_of(to * domains + g * CHUNK, 16), CHUNK), :],
@@ -173,24 +179,71 @@
     far = list(range(n // 2, n))
     close = list(range(1, n // 2))
     far_first = far + close
-    middle = (me >= n // 2 - cores) & (me < n // 2 + cores)
     pairs = [(g, k) for g in range(chunks) for k in far_first]
-    middle_early = [(0, k) for k in far_first]
+    first_pairs = [(0, k) for k in reversed(range(n - cores, n))]
+    middle_early = first_pairs + [(0, k) for k in far_first if k < n - cores]
+    middle_early += [(1, k) for k in range(n - cores, n) if chunks > 1]
     outer_early = [(g, k) for g in range(chunks) for k in close]
+    half = domains // 16
+
+    def start_near():
+        @pl.when(has_right)
+        def _():
+            for copy in near_copies(0):
+                copy.start()
+
+        @pl.when(has_left)
+        def _():
+            for copy in near_copies(2):
+                copy.start()
+
+    def start_own():
+        for g in range(chunks):
+            source, place = in_views(me, g)
+            pltpu.make_async_copy(source, place, in_recv.at[g]).start()
 
     @pl.when(middle)
     def _():
-        for g, k in middle_early:
+        small[0].wait()
+        with jax.named_scope("w_middle"):
+            pl.semaphore_wait(barrier, span - 1)
+        if staged:
+            chip_copy(chips - 1).start()
+        for g, k in first_pairs:
             in_copy(g, k).start()
-
-    @pl.when(jnp.logical_not(middle))
-    def _():
+        start_own()
+        for copy in small[1:]:
+            copy.wait()
+        marking(0, half)
+        with jax.named_scope("w_entered"):
+            pl.semaphore_wait(entered, 1)
+        for j in range(1, chips - 1):
+            chip_copy(j).start()
+        start_near()
+        for g, k in middle_early[len(first_pairs):]:
+            in_copy(g, k).start()
+
+    @pl.when(outer)
+    def _():
+        with jax.named_scope("w_barrier"):
+            pl.semaphore_wait(barrier, peers - 1)
+        if staged:
+            @pl.when((me >= low + span) & (me < low + span + cores))
+            def _():
+                for j in range(1, 3):
+                    pl.semaphore_signal(
+                        entered, inc=1, device_id={"member": me - j * cores}, device_id_type=MESH
+                    )
+        small[0].wait()
+        for j in range(1, chips):
+            chip_copy(j).start()
+        start_near()
         for g, k in outer_early:
             in_copy(g, k).start()
-
-    for g in range(chunks):
-        source, place = in_views(me, g)
-        pltpu.make_async_copy(source, place, in_recv.at[g]).start()
+        start_own()
+        for copy in small[1:]:
+            copy.wait()
+        marking(0, half)
 
     for side, missing in ((0, space == 0), (2, space == spaces - 1)):
         @pl.when(missing)
@@ -199,10 +252,7 @@
             for single in singles[side]:
                 single[...] = jnp.ones(single.shape, BF16)
 
-    for copy in small[1:]:
-        copy.wait()
-    with jax.named_scope("marks"):
-        lax.fori_loop(0, domains // 8, mark, 0)
+    marking(half, domains // 8)
 
     with jax.named_scope("w_chip"):
         if chips > 1:
@@ -337,7 +387,7 @@
             landed(others, sum_recv.at[0])
         sums_all = lax.fori_loop(1, peers, add_sum, moved[...])
 
-    @pl.when(jnp.logical_not(middle))
+    @pl.when(outer)
     def _():
         for g, k in pairs:
             if (g, k) not in outer_early:
@@ -438,6 +488,7 @@
         in_specs=[anywhere] * 6,
         out_specs=vmem,
         scratch_shapes=[
+            pltpu.SemaphoreType.REGULAR,
             pltpu.VMEM((patch,), BF16),
             pltpu.VMEM((patch,), BF16),
             pltpu.VMEM((patch,), BF16),

time: 93.3 us -> 90.3 us (0.968)
  Pallas kernels: 91.4 us -> 88.2 us
    pallas_call x1, Pallas kernels: 91.4 us -> 88.2 us  [per_device(): pl.pallas_call(functools.partial(analyse_kernel, n, spaces, halo, obs_cou...]
where the time goes in v4:
time: 90.3 us; the launch traced here: 89.4 us
  Pallas kernels  88.2 us (98%)
  local copies, waits for them, and re-layouts  1.27 us (1%)
    pallas_call x1, Pallas kernels, per_device(): pl.pallas_call(functools.partial(analyse_kernel, n, spaces, halo, obs_cou...  88.2 us

profile of v4, /device:TPU:10, one launch (start us, length us, event | category | flops | bytes accessed | tf_op | source)
XLA Modules:
  0.0 89.4 jit_solution(12984487172106537182)
XLA Ops:
  0.0 88.2 %analyse.1 = bf16[10,384,256]{2,1,0:T(8,128)(2,1)S(1)} custom-call(bf16[10,384,256]{2,1,0:T(8,128)(2,1)} %x.1, bf16[10,384]{1,0:T(8,128)(2,1)} %sensors_in.1, bf16[384]{0:T(512)(128)(2,1)} %readings_in.1, bf16[384]{0:T(512)(128)(2,1)} %noises_in.1, s32[384,128]{1,0:T(8,128)} %lists_in.1, s32[384]{0:T(512)} %tiers_in.1), custom_call_target="tpu_custom_call" | custom-call | tf_op jit(solution)/shard_map/analyse/pallas_call | solution.py:485
  88.2 1.3 %copy.8 = bf16[10,384,256]{2,1,0:T(8,128)(2,1)} copy(bf16[10,384,256]{2,1,0:T(8,128)(2,1)S(1)} %analyse.1) | data formatting | bytes 3932160

commit v5 on v4

--- a/solution.py
+++ b/solution.py
@@ -46,7 +46,7 @@
 def analyse_kernel(
     n, spaces, halo, obs_count, x, sensors_in, readings_in, noises_in, lists_in, tiers_in,
     out,
-    entered, readings, noises, left_readings, left_noises, right_readings, right_noises, lists, tiers, small_sem, incoming, updated, gathered, full, anoms, anoms_t, marks, weights, gram, target, trans,
+    entered, readings, noises, left_readings, left_noises, right_readings, right_noises, lists, tiers, small_sem, stage_sem, stage, incoming, updated, gathered, full, anoms, anoms_t, marks, weights, gram, target, trans,
     moved, sums,
     in_send, in_recv, out_send, out_recv, near_send, near_recv, chip_send, chip_recv, side_send, side_recv, sum_send, sum_recv,
 ):
@@ -75,6 +75,12 @@
     def central(member):
         return (member >= low) & (member < low + span)
 
+    def in_views(to, g):
+        return (
+            x.at[:, pl.ds(pl.multiple_of(to * domains + g * CHUNK, 16), CHUNK), :],
+            incoming.at[pl.ds(me * members, members), pl.ds(g * CHUNK, CHUNK), :],
+        )
+
     middle = central(me)
     outer = jnp.logical_not(middle)
     barrier = pltpu.get_barrier_semaphore()
@@ -88,6 +94,12 @@
         for k in range(1, span):
             other = low + lax.rem(me - low + k, span)
             pl.semaphore_signal(barrier, inc=1, device_id={"member": other}, device_id_type=MESH)
+        for i in range(cores):
+            source, _ = in_views(partner(me, n - 1 - i, n), 0)
+            pltpu.make_async_copy(source, stage.at[i], stage_sem.at[0]).start()
+
+    half_chips = chips // 2
+    upper = chip >= half_chips
 
     small = [
         pltpu.make_async_copy(source, place, small_sem.at[i])
@@ -133,12 +145,26 @@
     def to_space(side):
         return lax.rem(space + 1 - side + spaces, spaces)
 
-    def chip_copy(j):
+    def slot_copy(other, half):
         place = gathered.at[1, slot(me)]
-        other = partner(chip, j, chips) * cores + core
         return pltpu.make_async_remote_copy(
-            place, place, chip_send.at[0], chip_recv.at[0],
-            device_id={"member": other}, device_id_type=MESH,
+            place, place, chip_send.at[0], chip_recv.at[half],
+            device_id={"member": other * cores + core}, device_id_type=MESH,
+        )
+
+    def near_slots():
+        for j in range(1, half_chips if staged else chips):
+            slot_copy(partner(chip, j, chips), 0).start()
+
+    def cross_slot():
+        if staged:
+            slot_copy(half_chips - upper.astype(jnp.int32), 1).start()
+
+    def relay_copy(j):
+        rows = pl.ds(core * chips + (1 - upper.astype(jnp.int32)) * half_chips, half_chips)
+        return pltpu.make_async_remote_copy(
+            gathered.at[1, rows], gathered.at[1, rows], chip_send.at[j], chip_recv.at[1],
+            device_id={"member": partner(chip, j, chips) * cores + core}, device_id_type=MESH,
         )
 
     singles = [(left_readings, left_noises), (readings, noises), (right_readings, right_noises)]
@@ -162,15 +188,10 @@
             device_id_type=MESH,
         )
 
-    def in_views(to, g):
-        return (
-            x.at[:, pl.ds(pl.multiple_of(to * domains + g * CHUNK, 16), CHUNK), :],
-            incoming.at[pl.ds(me * members, members), pl.ds(g * CHUNK, CHUNK), :],
-        )
-
-    def in_copy(g, k):
+    def in_copy(g, k, copied=None):
         to = partner(me, k, n)
         source, place = in_views(to, g)
+        source = source if copied is None else copied
         return pltpu.make_async_remote_copy(
             source, place, in_send.at[0], in_recv.at[g],
             device_id={"member": to}, device_id_type=MESH,
@@ -181,8 +202,9 @@
     far_first = far + close
     pairs = [(g, k) for g in range(chunks) for k in far_first]
     first_pairs = [(0, k) for k in reversed(range(n - cores, n))]
-    middle_early = first_pairs + [(0, k) for k in far_first if k < n - cores]
-    middle_early += [(1, k) for k in range(n - cores, n) if chunks > 1]
+    opposite = [(g, k) for g in range(1, chunks) for k in range(n - cores, n)]
+    relayed = [(0, k) for k in close]
+    middle_early = first_pairs + opposite + relayed
     outer_early = [(g, k) for g in range(chunks) for k in close]
     half = domains // 16
 
@@ -204,23 +226,24 @@
 
     @pl.when(middle)
     def _():
-        small[0].wait()
         with jax.named_scope("w_middle"):
             pl.semaphore_wait(barrier, span - 1)
-        if staged:
-            chip_copy(chips - 1).start()
-        for g, k in first_pairs:
-            in_copy(g, k).start()
+        with jax.named_scope("w_stage"):
+            landed(stage, stage_sem.at[0])
+        for i, (g, k) in enumerate(first_pairs):
+            in_copy(g, k, stage.at[i]).start()
+            if i == 0:
+                small[0].wait()
+                cross_slot()
         start_own()
         for copy in small[1:]:
             copy.wait()
         marking(0, half)
         with jax.named_scope("w_entered"):
             pl.semaphore_wait(entered, 1)
-        for j in range(1, chips - 1):
-            chip_copy(j).start()
+        near_slots()
         start_near()
-        for g, k in middle_early[len(first_pairs):]:
+        for g, k in opposite:
             in_copy(g, k).start()
 
     @pl.when(outer)
@@ -235,8 +258,8 @@
                         entered, inc=1, device_id={"member": me - j * cores}, device_id_type=MESH
                     )
         small[0].wait()
-        for j in range(1, chips):
-            chip_copy(j).start()
+        cross_slot()
+        near_slots()
         start_near()
         for g, k in outer_early:
             in_copy(g, k).start()
@@ -255,10 +278,18 @@
     marking(half, domains // 8)
 
     with jax.named_scope("w_chip"):
-        if chips > 1:
-            others = gathered.at[1, pl.ds(0, chips - 1)]
-            landed(others, chip_send.at[0])
-            landed(others, chip_recv.at[0])
+        if staged:
+            landed(gathered.at[1, pl.ds(0, half_chips)], chip_recv.at[1])
+
+            @pl.when(middle)
+            def _():
+                for j in range(1, half_chips):
+                    relay_copy(j).start()
+                for g, k in relayed:
+                    in_copy(g, k).start()
+        near = half_chips - 1 if staged else chips - 1
+        if near:
+            landed(gathered.at[1, pl.ds(0, near)], chip_recv.at[0])
 
     for t in range(1, cores):
         side_copy(1, t).start()
@@ -274,6 +305,14 @@
             side_copy(2, t).start()
 
     with jax.named_scope("w_side"):
+        sent = half_chips if staged else chips - 1
+        if sent:
+            landed(gathered.at[1, pl.ds(0, sent)], chip_send.at[0])
+        if staged:
+            @pl.when(middle)
+            def _():
+                for j in range(1, half_chips):
+                    relay_copy(j).wait_send()
         if cores > 1:
             others = gathered.at[1, pl.ds(0, n - chips)]
             landed(others, side_send.at[1])
@@ -497,7 +536,8 @@
             pltpu.VMEM((patch,), BF16),
             pltpu.VMEM((domains, obs_count), jnp.int32),
             pltpu.VMEM((patch,), jnp.int32),
-            dma((5,)),
+            dma((5,)), dma((1,)),
+            pltpu.VMEM((2 - n % 2, members, CHUNK, quantities), BF16),
             pltpu.VMEM((lines, domains, quantities), BF16),
             pltpu.VMEM((lines, domains, quantities), BF16),
             pltpu.VMEM((3, n, members, patch), BF16),
@@ -512,7 +552,7 @@
             pltpu.VMEM((1, LANES), F32),
             pltpu.VMEM((n * spaces, 1, LANES), F32),
             dma((1,)), dma((chunks,)), dma((1,)), dma((1,)),
-            dma((2, 2)), dma((2, 2)), dma((1,)), dma((1,)), dma((3,)), dma((3,)), dma((1,)), dma((1,)),
+            dma((2, 2)), dma((2, 2)), dma((max(n // 4, 1),)), dma((2,)), dma((3,)), dma((3,)), dma((1,)), dma((1,)),
         ],
         compiler_params=pltpu.CompilerParams(
             collective_id=0, has_side_effects=True, vmem_limit_bytes=40 << 20

time: 90.3 us -> 90.1 us (level)
  no operation moved by 1% of the time
where the time goes in v5:
time: 90.1 us; the launch traced here: 89.6 us
  Pallas kernels  88.3 us (98%)
  local copies, waits for them, and re-layouts  1.27 us (1%)
    pallas_call x1, Pallas kernels, per_device(): pl.pallas_call(functools.partial(analyse_kernel, n, spaces, halo, obs_cou...  88.3 us

profile of v5, /device:TPU:10, one launch (start us, length us, event | category | flops | bytes accessed | tf_op | source)
XLA Modules:
  0.0 89.6 jit_solution(17135868138978577483)
XLA Ops:
  0.0 88.3 %analyse.1 = bf16[10,384,256]{2,1,0:T(8,128)(2,1)S(1)} custom-call(bf16[10,384,256]{2,1,0:T(8,128)(2,1)} %x.1, bf16[10,384]{1,0:T(8,128)(2,1)} %sensors_in.1, bf16[384]{0:T(512)(128)(2,1)} %readings_in.1, bf16[384]{0:T(512)(128)(2,1)} %noises_in.1, s32[384,128]{1,0:T(8,128)} %lists_in.1, s32[384]{0:T(512)} %tiers_in.1), custom_call_target="tpu_custom_call" | custom-call | tf_op jit(solution)/shard_map/analyse/pallas_call | solution.py:524
  88.3 1.3 %copy.8 = bf16[10,384,256]{2,1,0:T(8,128)(2,1)} copy(bf16[10,384,256]{2,1,0:T(8,128)(2,1)S(1)} %analyse.1) | data formatting | bytes 3932160

commit v6 on v5

--- a/solution.py
+++ b/solution.py
@@ -91,12 +91,10 @@
 
     @pl.when(middle)
     def _():
-        for k in range(1, span):
-            other = low + lax.rem(me - low + k, span)
-            pl.semaphore_signal(barrier, inc=1, device_id={"member": other}, device_id_type=MESH)
-        for i in range(cores):
-            source, _ = in_views(partner(me, n - 1 - i, n), 0)
-            pltpu.make_async_copy(source, stage.at[i], stage_sem.at[0]).start()
+        other = partner(me, n - cores, n)
+        pl.semaphore_signal(barrier, inc=1, device_id={"member": other}, device_id_type=MESH)
+        source, _ = in_views(other, 0)
+        pltpu.make_async_copy(source, stage, stage_sem.at[0]).start()
 
     half_chips = chips // 2
     upper = chip >= half_chips
@@ -201,10 +199,10 @@
     close = list(range(1, n // 2))
     far_first = far + close
     pairs = [(g, k) for g in range(chunks) for k in far_first]
-    first_pairs = [(0, k) for k in reversed(range(n - cores, n))]
-    opposite = [(g, k) for g in range(1, chunks) for k in range(n - cores, n)]
+    facing = [(g, n - cores) for g in range(chunks)]
+    crossed = [(g, k) for g in range(chunks) for k in range(n - cores + 1, n)]
     relayed = [(0, k) for k in close]
-    middle_early = first_pairs + opposite + relayed
+    middle_early = facing + crossed + relayed
     outer_early = [(g, k) for g in range(chunks) for k in close]
     half = domains // 16
 
@@ -227,14 +225,14 @@
     @pl.when(middle)
     def _():
         with jax.named_scope("w_middle"):
-            pl.semaphore_wait(barrier, span - 1)
+            pl.semaphore_wait(barrier, 1)
         with jax.named_scope("w_stage"):
             landed(stage, stage_sem.at[0])
-        for i, (g, k) in enumerate(first_pairs):
-            in_copy(g, k, stage.at[i]).start()
-            if i == 0:
-                small[0].wait()
-                cross_slot()
+        in_copy(*facing[0], stage).start()
+        small[0].wait()
+        cross_slot()
+        for g, k in facing[1:]:
+            in_copy(g, k).start()
         start_own()
         for copy in small[1:]:
             copy.wait()
@@ -243,7 +241,7 @@
             pl.semaphore_wait(entered, 1)
         near_slots()
         start_near()
-        for g, k in opposite:
+        for g, k in crossed:
             in_copy(g, k).start()
 
     @pl.when(outer)
@@ -416,8 +414,17 @@
             gram[c] = prod[:lines, :LANES] + prod[:lines, LANES:] + prod[lines:, :LANES]
         return carry
 
-    with jax.named_scope('gram'):
-        lax.fori_loop(0, domains // 2, gram_group, 0)
+    with jax.named_scope("gram"):
+        lax.fori_loop(0, domains // 4, gram_group, 0)
+
+    @pl.when(outer)
+    def _():
+        for g, k in pairs:
+            if (g, k) not in outer_early:
+                in_copy(g, k).start()
+
+    with jax.named_scope("gram"):
+        lax.fori_loop(domains // 4, domains // 2, gram_group, 0)
 
     with jax.named_scope("w_sums"):
         if peers > 1:
@@ -425,12 +432,6 @@
             landed(others, sum_send.at[0])
             landed(others, sum_recv.at[0])
         sums_all = lax.fori_loop(1, peers, add_sum, moved[...])
-
-    @pl.when(outer)
-    def _():
-        for g, k in pairs:
-            if (g, k) not in outer_early:
-                in_copy(g, k).start()
 
     scale = sums_all[:, 1:2] / sums_all[:, 0:1]
     eye = jnp.where(
@@ -469,14 +470,21 @@
             trans[c] = w.astype(BF16)
         return carry
 
+    if staged:
+        beyond = list(range(half_chips, chips)) + list(range(1, half_chips))
+        receivers = [
+            partner(chip, j, chips) * cores + c for j in beyond for c in reversed(range(cores))
+        ] + [chip * cores + lax.rem(core + t, cores) for t in range(1, cores)]
+    else:
+        receivers = [partner(me, k, n) for k in far_first]
+
     def out_views(to, g):
         return (
             updated.at[pl.ds(to * members, members), pl.ds(g * CHUNK, CHUNK), :],
             out.at[:, pl.ds(pl.multiple_of(me * domains + g * CHUNK, 16), CHUNK), :],
         )
 
-    def out_copy(g, k):
-        to = partner(me, k, n)
+    def out_copy(g, to):
         source, place = out_views(to, g)
         return pltpu.make_async_remote_copy(
             source, place, out_send.at[0], out_recv.at[0],
@@ -496,16 +504,17 @@
         ]
         results = jnp.stack(results, axis=0)
         updated[:, g * CHUNK : (g + 1) * CHUNK, :] = jnp.swapaxes(results, 0, 1).astype(BF16)
-        for k in far_first:
-            out_copy(g, k).start()
+        for to in receivers:
+            out_copy(g, to).start()
         source, place = out_views(me, g)
         pltpu.make_async_copy(source, place, out_recv.at[0]).start()
 
     with jax.named_scope("w_out"):
+        landed(out, out_recv.at[0])
+    with jax.named_scope("w_sent"):
         if n > 1:
             landed(x.at[:, pl.ds(0, patch - domains), :], in_send.at[0])
             landed(updated.at[pl.ds(0, lines - members)], out_send.at[0])
-        landed(out, out_recv.at[0])
 
 
 def per_device(trials, sensors, readings, noises, lists, tiers):
@@ -537,7 +546,7 @@
             pltpu.VMEM((domains, obs_count), jnp.int32),
             pltpu.VMEM((patch,), jnp.int32),
             dma((5,)), dma((1,)),
-            pltpu.VMEM((2 - n % 2, members, CHUNK, quantities), BF16),
+            pltpu.VMEM((members, CHUNK, quantities), BF16),
             pltpu.VMEM((lines, domains, quantities), BF16),
             pltpu.VMEM((lines, domains, quantities), BF16),
             pltpu.VMEM((3, n, members, patch), BF16),

time: 90.1 us -> 90 us (level)
  no operation moved by 1% of the time
where the time goes in v6:
time: 90 us; the launch traced here: 89.9 us
  Pallas kernels  88.6 us (98%)
  local copies, waits for them, and re-layouts  1.27 us (1%)
    pallas_call x1, Pallas kernels, per_device(): pl.pallas_call(functools.partial(analyse_kernel, n, spaces, halo, obs_cou...  88.6 us

profile of v6, /device:TPU:10, one launch (start us, length us, event | category | flops | bytes accessed | tf_op | source)
XLA Modules:
  0.0 89.9 jit_solution(16717647639852910562)
XLA Ops:
  0.0 88.6 %analyse.1 = bf16[10,384,256]{2,1,0:T(8,128)(2,1)S(1)} custom-call(bf16[10,384,256]{2,1,0:T(8,128)(2,1)} %x.1, bf16[10,384]{1,0:T(8,128)(2,1)} %sensors_in.1, bf16[384]{0:T(512)(128)(2,1)} %readings_in.1, bf16[384]{0:T(512)(128)(2,1)} %noises_in.1, s32[384,128]{1,0:T(8,128)} %lists_in.1, s32[384]{0:T(512)} %tiers_in.1), custom_call_target="tpu_custom_call" | custom-call | tf_op jit(solution)/shard_map/analyse/pallas_call | solution.py:533
  88.6 1.3 %copy.8 = bf16[10,384,256]{2,1,0:T(8,128)(2,1)} copy(bf16[10,384,256]{2,1,0:T(8,128)(2,1)S(1)} %analyse.1) | data formatting | bytes 3932160

commit v7 on v6

--- a/solution.py
+++ b/solution.py
@@ -81,6 +81,8 @@
             incoming.at[pl.ds(me * members, members), pl.ds(g * CHUNK, CHUNK), :],
         )
 
+    lead = max(members // 5, 1)
+    stage_parts = [pl.ds(0, lead), pl.ds(lead, members - lead)]
     middle = central(me)
     outer = jnp.logical_not(middle)
     barrier = pltpu.get_barrier_semaphore()
@@ -94,7 +96,8 @@
         other = partner(me, n - cores, n)
         pl.semaphore_signal(barrier, inc=1, device_id={"member": other}, device_id_type=MESH)
         source, _ = in_views(other, 0)
-        pltpu.make_async_copy(source, stage, stage_sem.at[0]).start()
+        for i, rows in enumerate(stage_parts):
+            pltpu.make_async_copy(source.at[rows], stage.at[rows], stage_sem.at[i]).start()
 
     half_chips = chips // 2
     upper = chip >= half_chips
@@ -186,10 +189,11 @@
             device_id_type=MESH,
         )
 
-    def in_copy(g, k, copied=None):
+    def in_copy(g, k, rows=None):
         to = partner(me, k, n)
         source, place = in_views(to, g)
-        source = source if copied is None else copied
+        if rows is not None:
+            source, place = stage.at[rows], place.at[rows]
         return pltpu.make_async_remote_copy(
             source, place, in_send.at[0], in_recv.at[g],
             device_id={"member": to}, device_id_type=MESH,
@@ -226,9 +230,9 @@
     def _():
         with jax.named_scope("w_middle"):
             pl.semaphore_wait(barrier, 1)
-        with jax.named_scope("w_stage"):
-            landed(stage, stage_sem.at[0])
-        in_copy(*facing[0], stage).start()
+        for i, rows in enumerate(stage_parts):
+            landed(stage.at[rows], stage_sem.at[i])
+            in_copy(*facing[0], rows).start()
         small[0].wait()
         cross_slot()
         for g, k in facing[1:]:
@@ -545,7 +549,7 @@
             pltpu.VMEM((patch,), BF16),
             pltpu.VMEM((domains, obs_count), jnp.int32),
             pltpu.VMEM((patch,), jnp.int32),
-            dma((5,)), dma((1,)),
+            dma((5,)), dma((2,)),
             pltpu.VMEM((members, CHUNK, quantities), BF16),
             pltpu.VMEM((lines, domains, quantities), BF16),
             pltpu.VMEM((lines, domains, quantities), BF16),

time: 90 us -> 89.9 us (level)
  no operation moved by 1% of the time
where the time goes in v7:
time: 89.9 us; the launch traced here: 89.7 us
  Pallas kernels  88.5 us (98%)
  local copies, waits for them, and re-layouts  1.27 us (1%)
    pallas_call x1, Pallas kernels, per_device(): pl.pallas_call(functools.partial(analyse_kernel, n, spaces, halo, obs_cou...  88.5 us

profile of v7, /device:TPU:10, one launch (start us, length us, event | category | flops | bytes accessed | tf_op | source)
XLA Modules:
  0.0 89.7 jit_solution(13680805303373242607)
XLA Ops:
  0.0 88.5 %analyse.1 = bf16[10,384,256]{2,1,0:T(8,128)(2,1)S(1)} custom-call(bf16[10,384,256]{2,1,0:T(8,128)(2,1)} %x.1, bf16[10,384]{1,0:T(8,128)(2,1)} %sensors_in.1, bf16[384]{0:T(512)(128)(2,1)} %readings_in.1, bf16[384]{0:T(512)(128)(2,1)} %noises_in.1, s32[384,128]{1,0:T(8,128)} %lists_in.1, s32[384]{0:T(512)} %tiers_in.1), custom_call_target="tpu_custom_call" | custom-call | tf_op jit(solution)/shard_map/analyse/pallas_call | solution.py:537
  88.5 1.3 %copy.8 = bf16[10,384,256]{2,1,0:T(8,128)(2,1)} copy(bf16[10,384,256]{2,1,0:T(8,128)(2,1)S(1)} %analyse.1) | data formatting | bytes 3932160

commit v8 on v7

--- a/solution.py
+++ b/solution.py
@@ -46,7 +46,7 @@
 def analyse_kernel(
     n, spaces, halo, obs_count, x, sensors_in, readings_in, noises_in, lists_in, tiers_in,
     out,
-    entered, readings, noises, left_readings, left_noises, right_readings, right_noises, lists, tiers, small_sem, stage_sem, stage, incoming, updated, gathered, full, anoms, anoms_t, marks, weights, gram, target, trans,
+    entered, sensors, readings, noises, left_readings, left_noises, right_readings, right_noises, lists, tiers, small_sem, stage_sem, stage, incoming, updated, gathered, full, anoms, anoms_t, marks, weights, gram, target, trans,
     moved, sums,
     in_send, in_recv, out_send, out_recv, near_send, near_recv, chip_send, chip_recv, side_send, side_recv, sum_send, sum_recv,
 ):
@@ -106,7 +106,7 @@
         pltpu.make_async_copy(source, place, small_sem.at[i])
         for i, (source, place) in enumerate(
             [
-                (sensors_in, gathered.at[1, slot(me)]), (readings_in, readings), (noises_in, noises),
+                (sensors_in, sensors), (readings_in, readings), (noises_in, noises),
                 (lists_in.at[pl.ds(pl.multiple_of(me * domains, 8), domains)], lists),
                 (tiers_in, tiers),
             ]
@@ -145,6 +145,17 @@
 
     def to_space(side):
         return lax.rem(space + 1 - side + spaces, spaces)
+
+    strips = patch // LANES
+
+    def pack():
+        small[0].wait()
+        values = sensors[...].astype(F32)
+        rows = [values[:, LANES * t : LANES * (t + 1)] for t in range(strips)]
+        spare = gathered.shape[2] - members * strips
+        if spare:
+            rows.append(jnp.zeros((spare, LANES), F32))
+        gathered[1, slot(me)] = jnp.concatenate(rows, axis=0).astype(BF16)
 
     def slot_copy(other, half):
         place = gathered.at[1, slot(me)]
@@ -233,7 +244,7 @@
         for i, rows in enumerate(stage_parts):
             landed(stage.at[rows], stage_sem.at[i])
             in_copy(*facing[0], rows).start()
-        small[0].wait()
+        pack()
         cross_slot()
         for g, k in facing[1:]:
             in_copy(g, k).start()
@@ -250,6 +261,7 @@
 
     @pl.when(outer)
     def _():
+        pack()
         with jax.named_scope("w_barrier"):
             pl.semaphore_wait(barrier, peers - 1)
         if staged:
@@ -259,7 +271,6 @@
                     pl.semaphore_signal(
                         entered, inc=1, device_id={"member": me - j * cores}, device_id_type=MESH
                     )
-        small[0].wait()
         cross_slot()
         near_slots()
         start_near()
@@ -340,9 +351,12 @@
 
     for side in range(3):
         for s in range(n):
-            full[members * s : members * (s + 1), patch * side : patch * (side + 1)] = (
-                gathered[side, s % cores * chips + s // cores].astype(F32)
-            )
+            rows = gathered[side, s % cores * chips + s // cores].astype(F32)
+            for t in range(strips):
+                at = patch * side + LANES * t
+                full[members * s : members * (s + 1), at : at + LANES] = (
+                    rows[members * t : members * (t + 1)]
+                )
         for i, single in enumerate(singles[side]):
             full[lines + i : lines + i + 1, patch * side : patch * (side + 1)] = (
                 single[...].astype(F32)[None]
@@ -532,6 +546,7 @@
     width = -(-(domains + 2 * halo) // 256) * 256
     vmem = pl.BlockSpec(memory_space=pltpu.VMEM)
     anywhere = pl.BlockSpec(memory_space=pltpu.HBM)
+    packed = -(-members * (patch // LANES) // 16) * 16
     full_rows = -(-(lines + 2) // 8) * 8
     dma = pltpu.SemaphoreType.DMA
     return pl.pallas_call(
@@ -541,6 +556,7 @@
         out_specs=vmem,
         scratch_shapes=[
             pltpu.SemaphoreType.REGULAR,
+            pltpu.VMEM((members, patch), BF16),
             pltpu.VMEM((patch,), BF16),
             pltpu.VMEM((patch,), BF16),
             pltpu.VMEM((patch,), BF16),
@@ -553,7 +569,7 @@
             pltpu.VMEM((members, CHUNK, quantities), BF16),
             pltpu.VMEM((lines, domains, quantities), BF16),
             pltpu.VMEM((lines, domains, quantities), BF16),
-            pltpu.VMEM((3, n, members, patch), BF16),
+            pltpu.VMEM((3, n, packed, LANES), BF16),
             pltpu.VMEM((full_rows, 3 * patch), F32),
             pltpu.VMEM((lines, width), F32),
             pltpu.VMEM((width, 2 * LANES), BF16),

time: 89.9 us -> 89.8 us (level)
  no operation moved by 1% of the time
where the time goes in v8:
time: 89.8 us; the launch traced here: 89.6 us
  Pallas kernels  88.3 us (98%)
  local copies, waits for them, and re-layouts  1.27 us (1%)
    pallas_call x1, Pallas kernels, per_device(): pl.pallas_call(functools.partial(analyse_kernel, n, spaces, halo, obs_cou...  88.3 us

profile of v8, /device:TPU:10, one launch (start us, length us, event | category | flops | bytes accessed | tf_op | source)
XLA Modules:
  0.0 89.6 jit_solution(8644906123835890989)
XLA Ops:
  0.0 88.3 %analyse.1 = bf16[10,384,256]{2,1,0:T(8,128)(2,1)S(1)} custom-call(bf16[10,384,256]{2,1,0:T(8,128)(2,1)} %x.1, bf16[10,384]{1,0:T(8,128)(2,1)} %sensors_in.1, bf16[384]{0:T(512)(128)(2,1)} %readings_in.1, bf16[384]{0:T(512)(128)(2,1)} %noises_in.1, s32[384,128]{1,0:T(8,128)} %lists_in.1, s32[384]{0:T(512)} %tiers_in.1), custom_call_target="tpu_custom_call" | custom-call | tf_op jit(solution)/shard_map/analyse/pallas_call | solution.py:552
  88.3 1.3 %copy.8 = bf16[10,384,256]{2,1,0:T(8,128)(2,1)} copy(bf16[10,384,256]{2,1,0:T(8,128)(2,1)S(1)} %analyse.1) | data formatting | bytes 3932160

commit v9 on v8

--- a/solution.py
+++ b/solution.py
@@ -48,7 +48,7 @@
     out,
     entered, sensors, readings, noises, left_readings, left_noises, right_readings, right_noises, lists, tiers, small_sem, stage_sem, stage, incoming, updated, gathered, full, anoms, anoms_t, marks, weights, gram, target, trans,
     moved, sums,
-    in_send, in_recv, out_send, out_recv, near_send, near_recv, chip_send, chip_recv, side_send, side_recv, sum_send, sum_recv,
+    in_send, in_recv, out_recv, near_recv, chip_send, chip_recv, side_send, side_recv, sum_recv,
 ):
     me = lax.axis_index("member")
     space = lax.axis_index("space")
@@ -160,7 +160,7 @@
     def slot_copy(other, half):
         place = gathered.at[1, slot(me)]
         return pltpu.make_async_remote_copy(
-            place, place, chip_send.at[0], chip_recv.at[half],
+            place, place, small_sem.at[0], chip_recv.at[half],
             device_id={"member": other * cores + core}, device_id_type=MESH,
         )
 
@@ -175,7 +175,7 @@
     def relay_copy(j):
         rows = pl.ds(core * chips + (1 - upper.astype(jnp.int32)) * half_chips, half_chips)
         return pltpu.make_async_remote_copy(
-            gathered.at[1, rows], gathered.at[1, rows], chip_send.at[j], chip_recv.at[1],
+            gathered.at[1, rows], gathered.at[1, rows], chip_send.at[j - 1], chip_recv.at[1],
             device_id={"member": partner(chip, j, chips) * cores + core}, device_id_type=MESH,
         )
 
@@ -185,7 +185,7 @@
         index = side // 2
         return [
             pltpu.make_async_remote_copy(
-                source, place, near_send.at[index, i], near_recv.at[index, i],
+                source, place, small_sem.at[1 + 2 * index + i], near_recv.at[index, i],
                 device_id={"space": to_space(side)}, device_id_type=MESH,
             )
             for i, (source, place) in enumerate(zip((readings_in, noises_in), singles[side]))
@@ -273,12 +273,12 @@
                     )
         cross_slot()
         near_slots()
-        start_near()
         for g, k in outer_early:
             in_copy(g, k).start()
         start_own()
         for copy in small[1:]:
             copy.wait()
+        start_near()
         marking(0, half)
 
     for side, missing in ((0, space == 0), (2, space == spaces - 1)):
@@ -320,7 +320,7 @@
     with jax.named_scope("w_side"):
         sent = half_chips if staged else chips - 1
         if sent:
-            landed(gathered.at[1, pl.ds(0, sent)], chip_send.at[0])
+            landed(gathered.at[1, pl.ds(0, sent)], small_sem.at[0])
         if staged:
             @pl.when(middle)
             def _():
@@ -399,7 +399,7 @@
 
     def sum_copy(k):
         return pltpu.make_async_remote_copy(
-            moved, sums.at[k], sum_send.at[0], sum_recv.at[0],
+            moved, sums.at[k], side_send.at[1], sum_recv.at[0],
             device_id=peer(k), device_id_type=MESH,
         )
 
@@ -447,7 +447,7 @@
     with jax.named_scope("w_sums"):
         if peers > 1:
             others = sums.at[pl.ds(1, peers - 1)]
-            landed(others, sum_send.at[0])
+            landed(others, side_send.at[1])
             landed(others, sum_recv.at[0])
         sums_all = lax.fori_loop(1, peers, add_sum, moved[...])
 
@@ -505,7 +505,7 @@
     def out_copy(g, to):
         source, place = out_views(to, g)
         return pltpu.make_async_remote_copy(
-            source, place, out_send.at[0], out_recv.at[0],
+            source, place, side_send.at[0], out_recv.at[0],
             device_id={"member": to}, device_id_type=MESH,
         )
 
@@ -532,7 +532,7 @@
     with jax.named_scope("w_sent"):
         if n > 1:
             landed(x.at[:, pl.ds(0, patch - domains), :], in_send.at[0])
-            landed(updated.at[pl.ds(0, lines - members)], out_send.at[0])
+            landed(updated.at[pl.ds(0, lines - members)], side_send.at[0])
 
 
 def per_device(trials, sensors, readings, noises, lists, tiers):
@@ -580,8 +580,8 @@
             pltpu.VMEM((domains, lines, LANES), BF16),
             pltpu.VMEM((1, LANES), F32),
             pltpu.VMEM((n * spaces, 1, LANES), F32),
-            dma((1,)), dma((chunks,)), dma((1,)), dma((1,)),
-            dma((2, 2)), dma((2, 2)), dma((max(n // 4, 1),)), dma((2,)), dma((3,)), dma((3,)), dma((1,)), dma((1,)),
+            dma((1,)), dma((chunks,)), dma((1,)),
+            dma((2, 2)), dma((max(n // 4 - 1, 1),)), dma((2,)), dma((3,)), dma((3,)), dma((1,)),
         ],
         compiler_params=pltpu.CompilerParams(
             collective_id=0, has_side_effects=True, vmem_limit_bytes=40 << 20

time: 89.8 us -> 89.7 us (level)
  no operation moved by 1% of the time
where the time goes in v9:
time: 89.7 us; the launch traced here: 89.5 us
  Pallas kernels  88.2 us (98%)
  local copies, waits for them, and re-layouts  1.27 us (1%)
    pallas_call x1, Pallas kernels, per_device(): pl.pallas_call(functools.partial(analyse_kernel, n, spaces, halo, obs_cou...  88.2 us

profile of v9, /device:TPU:10, one launch (start us, length us, event | category | flops | bytes accessed | tf_op | source)
XLA Modules:
  0.0 89.5 jit_solution(9963718267925190340)
XLA Ops:
  0.0 88.2 %analyse.1 = bf16[10,384,256]{2,1,0:T(8,128)(2,1)S(1)} custom-call(bf16[10,384,256]{2,1,0:T(8,128)(2,1)} %x.1, bf16[10,384]{1,0:T(8,128)(2,1)} %sensors_in.1, bf16[384]{0:T(512)(128)(2,1)} %readings_in.1, bf16[384]{0:T(512)(128)(2,1)} %noises_in.1, s32[384,128]{1,0:T(8,128)} %lists_in.1, s32[384]{0:T(512)} %tiers_in.1), custom_call_target="tpu_custom_call" | custom-call | tf_op jit(solution)/shard_map/analyse/pallas_call | solution.py:552
  88.2 1.3 %copy.8 = bf16[10,384,256]{2,1,0:T(8,128)(2,1)} copy(bf16[10,384,256]{2,1,0:T(8,128)(2,1)S(1)} %analyse.1) | data formatting | bytes 3932160

commit v10 on v9

--- a/solution.py
+++ b/solution.py
@@ -81,7 +81,7 @@
             incoming.at[pl.ds(me * members, members), pl.ds(g * CHUNK, CHUNK), :],
         )
 
-    lead = max(members // 5, 1)
+    lead = 1
     stage_parts = [pl.ds(0, lead), pl.ds(lead, members - lead)]
     middle = central(me)
     outer = jnp.logical_not(middle)
@@ -261,7 +261,6 @@
 
     @pl.when(outer)
     def _():
-        pack()
         with jax.named_scope("w_barrier"):
             pl.semaphore_wait(barrier, peers - 1)
         if staged:
@@ -271,6 +270,7 @@
                     pl.semaphore_signal(
                         entered, inc=1, device_id={"member": me - j * cores}, device_id_type=MESH
                     )
+        pack()
         cross_slot()
         near_slots()
         for g, k in outer_early:

time: 89.7 us -> 89.7 us (level)
  no operation moved by 1% of the time
where the time goes in v10:
time: 89.7 us; the launch traced here: 89.6 us
  Pallas kernels  88.3 us (98%)
  local copies, waits for them, and re-layouts  1.27 us (1%)
    pallas_call x1, Pallas kernels, per_device(): pl.pallas_call(functools.partial(analyse_kernel, n, spaces, halo, obs_cou...  88.3 us

profile of v10, /device:TPU:10, one launch (start us, length us, event | category | flops | bytes accessed | tf_op | source)
XLA Modules:
  0.0 89.6 jit_solution(9513797631758565341)
XLA Ops:
  0.0 88.3 %analyse.1 = bf16[10,384,256]{2,1,0:T(8,128)(2,1)S(1)} custom-call(bf16[10,384,256]{2,1,0:T(8,128)(2,1)} %x.1, bf16[10,384]{1,0:T(8,128)(2,1)} %sensors_in.1, bf16[384]{0:T(512)(128)(2,1)} %readings_in.1, bf16[384]{0:T(512)(128)(2,1)} %noises_in.1, s32[384,128]{1,0:T(8,128)} %lists_in.1, s32[384]{0:T(512)} %tiers_in.1), custom_call_target="tpu_custom_call" | custom-call | tf_op jit(solution)/shard_map/analyse/pallas_call | solution.py:552
  88.3 1.3 %copy.8 = bf16[10,384,256]{2,1,0:T(8,128)(2,1)} copy(bf16[10,384,256]{2,1,0:T(8,128)(2,1)S(1)} %analyse.1) | data formatting | bytes 3932160

commit v11 on v10

--- a/solution.py
+++ b/solution.py
@@ -418,6 +418,12 @@
             if (g, k) not in middle_early:
                 in_copy(g, k).start()
 
+    @pl.when(outer)
+    def _():
+        for g, k in pairs:
+            if (g, k) not in outer_early:
+                in_copy(g, k).start()
+
     hi, lo = split(weight * innov)
     aims = jnp.dot(jnp.concatenate([hi, lo], axis=0), anoms_t[...], preferred_element_type=F32)
     target[...] = aims[:domains, :LANES] + aims[:domains, LANES:] + aims[domains:, :LANES]
@@ -434,12 +440,6 @@
 
     with jax.named_scope("gram"):
         lax.fori_loop(0, domains // 4, gram_group, 0)
-
-    @pl.when(outer)
-    def _():
-        for g, k in pairs:
-            if (g, k) not in outer_early:
-                in_copy(g, k).start()
 
     with jax.named_scope("gram"):
         lax.fori_loop(domains // 4, domains // 2, gram_group, 0)

time: 89.7 us -> 89.7 us (level)
  no operation moved by 1% of the time
where the time goes in v11:
time: 89.7 us; the launch traced here: 89.6 us
  Pallas kernels  88.3 us (98%)
  local copies, waits for them, and re-layouts  1.27 us (1%)
    pallas_call x1, Pallas kernels, per_device(): pl.pallas_call(functools.partial(analyse_kernel, n, spaces, halo, obs_cou...  88.3 us

profile of v11, /device:TPU:10, one launch (start us, length us, event | category | flops | bytes accessed | tf_op | source)
XLA Modules:
  0.0 89.6 jit_solution(8760021087734870046)
XLA Ops:
  0.0 88.3 %analyse.1 = bf16[10,384,256]{2,1,0:T(8,128)(2,1)S(1)} custom-call(bf16[10,384,256]{2,1,0:T(8,128)(2,1)} %x.1, bf16[10,384]{1,0:T(8,128)(2,1)} %sensors_in.1, bf16[384]{0:T(512)(128)(2,1)} %readings_in.1, bf16[384]{0:T(512)(128)(2,1)} %noises_in.1, s32[384,128]{1,0:T(8,128)} %lists_in.1, s32[384]{0:T(512)} %tiers_in.1), custom_call_target="tpu_custom_call" | custom-call | tf_op jit(solution)/shard_map/analyse/pallas_call | solution.py:552
  88.3 1.3 %copy.8 = bf16[10,384,256]{2,1,0:T(8,128)(2,1)} copy(bf16[10,384,256]{2,1,0:T(8,128)(2,1)S(1)} %analyse.1) | data formatting | bytes 3932160
